TPU v7x, 32 devices: a whole 2x2x4 slice. The times are simulated.
32 devices in a mesh: vox: 8 (over z, core), sta: 4 (over y, x).
Axes of the slice: x: 2, y: 2, z: 4, core: 2. Of those that a mesh axis runs over, the one named last changes fastest.
Arguments:
- green_tensor: bfloat16 [4, 6, 256, 1024], P('sta', None, None, 'vox'), may hold values from -0.078125 to 0.078125
- strain: bfloat16 [8, 6, 256, 1024], P('sta', None, None, 'vox'), may hold values from -6 to 6
- pair_events: int32 [4, 8], P('sta'), may hold values from -1 to 7, as said below
- pair_counts: int32 [4], P('sta'), may hold values from 6 to 8, as said below
- residuals: float32 [4, 8, 256], P('sta'), may hold values from -0.375 to 0.375
Outputs:
- kernel: float32 [1024], P(('vox', 'sta'))
Inputs may be any that keep to these rules, and one draw needn't show every extreme that they name: `pair_events`: within a station the live entries are distinct earthquakes; slots at or beyond the station's count hold -1. `pair_counts`: some station has exactly 8 live slots in every draw.
All inputs are finite; a program needn't handle non-finite values.
Results may differ from a plain program's by a relative error of at most 0.0029.
Values may be sent and summed in bfloat16 or wider, within the bound.
A program may use at most 64 MiB of HBM per device.

v0:
```python
import jax
import jax.numpy as jnp
from jax import lax
from jax.sharding import PartitionSpec as P


def for_sending(x):
    return jax.tree.map(lambda a: a.astype(jnp.bfloat16) if a.dtype == jnp.float32 else a, x)


def from_behind(x, axis, by):
    count = lax.axis_size(axis)
    return lax.ppermute(x, axis, [(i, (i + by) % count) for i in range(count)])


def toeplitz(wave):
    length = wave.shape[-1]
    leading = wave.shape[:-1]
    padded = jnp.concatenate([jnp.zeros(leading + (length,), wave.dtype), wave], axis=-1)
    flipped = jnp.flip(padded, axis=-1)
    reps = (1,) * len(leading) + (length,)
    tiled = jnp.tile(flipped, reps)
    width = 2 * length - 1
    trimmed = tiled[..., : length * width]
    shaped = trimmed.reshape(leading + (length, width))
    return shaped[..., length - 1 :]


def contribution(block, strain, base):
    green, events, counts, resid = block
    local = base + jnp.arange(strain.shape[0], dtype=jnp.int32)
    live = jnp.arange(events.shape[1], dtype=jnp.int32)[None, :] < counts[:, None]
    match = ((events[:, :, None] == local[None, None, :]) & live[:, :, None]).astype(jnp.float32)
    combined = jnp.einsum("spe,spt->set", match, resid, precision=lax.Precision.HIGHEST)
    matrix = toeplitz(combined).astype(jnp.bfloat16)
    conv = jnp.einsum("setu,ecuv->sectv", matrix, strain, preferred_element_type=jnp.float32)
    return jnp.sum(conv * green[:, None].astype(jnp.float32), axis=(0, 1, 2, 3))


def move_right(block):
    return jax.tree.map(
        lambda part, own: part.astype(own.dtype), from_behind(for_sending(block), "sta", 1), block
    )


def body(green_tensor, strain, pair_events, pair_counts, residuals):
    base = lax.axis_index("sta") * strain.shape[0]
    block = (green_tensor, pair_events, pair_counts, residuals)
    half = lax.axis_size("sta") // 2
    own = contribution(block, strain, base)

    def advance(turn, state):
        right_block, left_block, total = state
        right_block = move_right(right_block)
        left_block = jax.tree.map(
            lambda part, own: part.astype(own.dtype),
            from_behind(for_sending(left_block), "sta", -1),
            left_block,
        )
        total = (
            total + contribution(right_block, strain, base) + contribution(left_block, strain, base)
        )
        return (right_block, left_block, total)

    right_block, left_block, kernel = lax.fori_loop(0, half - 1, advance, (block, block, own))
    right_block = move_right(right_block)
    kernel = kernel + contribution(right_block, strain, base)
    return lax.psum_scatter(kernel, "sta", scatter_dimension=0, tiled=True)


def solution(mesh):
    in_specs = (
        P("sta", None, None, "vox"),
        P("sta", None, None, "vox"),
        P("sta", None),
        P("sta"),
        P("sta", None, None),
    )
    out_specs = P(("vox", "sta"))
    return jax.shard_map(body, mesh=mesh, in_specs=in_specs, out_specs=out_specs, check_vma=False)
```

profile of v0, /device:TPU:0, one launch (start us, length us, event | category | flops | bytes accessed | tf_op | source)
XLA Modules:
  0.0 57.3 jit_solution(2111566560230894561)
XLA Ops:
  0.0 0.8 %convert_element_type.72 = bf16[1,8,256]{2,1,0:T(8,128)(2,1)S(1)} convert(f32[1,8,256]{2,1,0:T(8,128)} %param.9) | non-fusion elementwise | flops 2048 | bytes 12288 | tf_op jit(solution)/shard_map/while/body/eval_jaxpr/convert_element_type | solution.py:8
  0.8 3.0 %collective-permute-start.2 = (bf16[1,8,256]{2,1,0:T(8,128)(2,1)S(1)}, bf16[1,8,256]{2,1,0:T(8,128)(2,1)S(1)}, u32[]{:S(2)}, u32[]{:S(2)}) collective-permute-start(bf16[1,8,256]{2,1,0:T(8,128)(2,1)S(1)} %convert_element_type.72), channel_id=1, source_target_pairs={{0,1},{1,2},{2,3},{3,0},{4,5},{5,6},{6,7},{7,4},{8,9},{9,10},{10,1... | collective-permute-start | bytes 12296 | tf_op jit(solution)/shard_map/while/body/eval_jaxpr/ppermute | solution.py:13
  3.8 1.0 %collective-permute-start.6 = (bf16[1,8,256]{2,1,0:T(8,128)(2,1)S(1)}, bf16[1,8,256]{2,1,0:T(8,128)(2,1)S(1)}, u32[]{:S(2)}, u32[]{:S(2)}) collective-permute-start(bf16[1,8,256]{2,1,0:T(8,128)(2,1)S(1)} %convert_element_type.72), channel_id=1, source_target_pairs={{0,3},{1,0},{2,1},{3,2},{4,7},{5,4},{6,5},{7,6},{8,11},{9,8},{10,9... | collective-permute-start | bytes 12296 | tf_op jit(solution)/shard_map/while/body/eval_jaxpr/ppermute | solution.py:13
  4.7 1.1 %collective-permute-start.1 = (s32[1]{0:T(128)}, s32[1]{0:T(128)}, u32[]{:S(2)}, u32[]{:S(2)}) collective-permute-start(s32[1]{0:T(128)} %param.8), channel_id=1, source_target_pairs={{0,1},{1,2},{2,3},{3,0},{4,5},{5,6},{6,7},{7,4},{8,9},{9,10},{10,1... | collective-permute-start | bytes 20 | tf_op jit(solution)/shard_map/while/body/eval_jaxpr/ppermute | solution.py:13
  5.8 2.4 %collective-permute-start = (s32[1,8]{1,0:T(1,128)}, s32[1,8]{1,0:T(1,128)S(1)}, u32[]{:S(2)}, u32[]{:S(2)}) collective-permute-start(s32[1,8]{1,0:T(1,128)} %param.7), channel_id=1, source_target_pairs={{0,1},{1,2},{2,3},{3,0},{4,5},{5,6},{6,7},{7,4},{8,9},{9,10},{10,1... | collective-permute-start | bytes 104 | tf_op jit(solution)/shard_map/while/body/eval_jaxpr/ppermute | solution.py:13
  8.2 0.6 %collective-permute-start.3 = (bf16[1,6,256,128]{3,2,1,0:T(8,128)(2,1)}, bf16[1,6,256,128]{3,2,1,0:T(8,128)(2,1)}, u32[]{:S(2)}, u32[]{:S(2)}) collective-permute-start(bf16[1,6,256,128]{3,2,1,0:T(8,128)(2,1)} %param.5), channel_id=1, source_target_pairs={{0,1},{1,2},{2,3},{3,0},{4,5},{5,6},{6,7},{7,4},{8,9},{9,10},{10,1... | collective-permute-start | bytes 1179656 | tf_op jit(solution)/shard_map/while/body/eval_jaxpr/ppermute | solution.py:13
  9.4 1.1 %bitcast_convert_fusion.3 = f32[6,256,128]{2,1,0:T(8,128)S(1)} fusion(bf16[1,6,256,128]{3,2,1,0:T(8,128)(2,1)} %param.5), kind=kLoop, calls=%fused_computation.15 | loop fusion | flops 196608 | bytes 1179648 | tf_op jit(solution)/shard_map/convert_element_type | solution.py:37
  10.5 0.2 convolution_bitcast_fusion.3
  10.7 0.4 rev.15
  11.2 0.4 tile.56
  11.5 0.4 slice.44
  11.9 0.0 copy-start.4
  11.9 1.3 %reshape.545 = bf16[1,2,256,511]{3,2,1,0:T(8,128)(2,1)S(1)} reshape(bf16[1,2,130816]{2,1,0:T(2,128)(2,1)S(1)} %slice.44) | data formatting | bytes 1046528 | tf_op jit(solution)/shard_map/reshape | solution.py:25
  13.3 0.0 copy-done.4
  13.3 0.6 %dynamic-slice = u32[1]{0:T(128)} dynamic-slice(u32[32]{0:T(128)S(1)} %copy-done.4, u32[]{:T(128)S(6)} %add.47), dynamic_slice_sizes={1} | dynamic-slice | bytes 12
  14.5 0.0 copy-done
  14.5 0.0 copy-start.1
  14.5 0.6 %fusion.3 = f32[128]{0:T(128)S(1)} fusion(bf16[2,6,256,128]{3,2,1,0:T(8,128)(2,1)S(1)} %copy-done, f32[6,256,128]{2,1,0:T(8,128)S(1)} %bitcast_convert_fusion.3, bf16[1,2,256,511]{3,2,1,0:T(8,128)(2,1)S(1)} %reshape.545), kind=kOutput, calls=%fused_computation.7 | convolution fusion | flops 202112896 | bytes 1835520 | tf_op jit(solution)/shard_map/setu,ecuv->sectv/dot_general | solution.py:36
  15.2 0.0 collective-permute-done.1
  15.2 2.4 %collective-permute-start.5 = (s32[1]{0:T(128)}, s32[1]{0:T(128)}, u32[]{:S(2)}, u32[]{:S(2)}) collective-permute-start(s32[1]{0:T(128)} %param.8), channel_id=1, source_target_pairs={{0,3},{1,0},{2,1},{3,2},{4,7},{5,4},{6,5},{7,6},{8,11},{9,8},{10,9... | collective-permute-start | bytes 20 | tf_op jit(solution)/shard_map/while/body/eval_jaxpr/ppermute | solution.py:13
  17.5 0.6 %iota_compare_fusion.2 = pred[8]{0:T(512)(128)(4,1)S(1)} fusion(s32[]{:T(128)} %bitcast.14), kind=kLoop, calls=%fused_computation.52 | loop fusion | flops 8 | bytes 12 | tf_op jit(solution)/shard_map/while/body/eval_jaxpr/lt | solution.py:32
  18.1 0.8 %collective-permute-done.5 = s32[1]{0:T(128)} collective-permute-done((s32[1]{0:T(128)}, s32[1]{0:T(128)}, u32[]{:S(2)}, u32[]{:S(2)}) %collective-permute-start.5) | collective-permute-done | bytes 36 | tf_op jit(solution)/shard_map/while/body/eval_jaxpr/ppermute | solution.py:13
  19.0 0.7 %iota_compare_fusion.1 = pred[8]{0:T(512)(128)(4,1)S(1)} fusion(s32[]{:T(128)} %bitcast.27), kind=kLoop, calls=%fused_computation.50 | loop fusion | flops 8 | bytes 12 | tf_op jit(solution)/shard_map/while/body/eval_jaxpr/lt | solution.py:32
  19.7 1.8 %collective-permute-start.9 = (s32[1]{0:T(128)}, s32[1]{0:T(128)}, u32[]{:S(2)}, u32[]{:S(2)}) collective-permute-start(s32[1]{0:T(128)} %collective-permute-done.1), channel_id=1, source_target_pairs={{0,1},{1,2},{2,3},{3,0},{4,5},{5,6},{6,7},{7,4},{8,9},{9,10},{10,1... | collective-permute-start | bytes 20 | tf_op jit(solution)/shard_map/ppermute | solution.py:13
  21.4 3.1 %collective-permute-done.9 = s32[1]{0:T(128)} collective-permute-done((s32[1]{0:T(128)}, s32[1]{0:T(128)}, u32[]{:S(2)}, u32[]{:S(2)}) %collective-permute-start.9) | collective-permute-done | bytes 36 | tf_op jit(solution)/shard_map/ppermute | solution.py:13
  24.6 2.0 %collective-permute-start.4 = (s32[1,8]{1,0:T(1,128)S(1)}, s32[1,8]{1,0:T(1,128)S(1)}, u32[]{:S(2)}, u32[]{:S(2)}) collective-permute-start(s32[1,8]{1,0:T(1,128)S(1)} %copy-done.3), channel_id=1, source_target_pairs={{0,3},{1,0},{2,1},{3,2},{4,7},{5,4},{6,5},{7,6},{8,11},{9,8},{10,9... | collective-permute-start | bytes 104 | tf_op jit(solution)/shard_map/while/body/eval_jaxpr/ppermute | solution.py:13
  26.6 0.7 %iota_compare_fusion = pred[8]{0:T(512)(128)(4,1)S(1)} fusion(s32[]{:T(128)} %bitcast.40), kind=kLoop, calls=%fused_computation.47 | loop fusion | flops 8 | bytes 12 | tf_op jit(solution)/shard_map/lt | solution.py:32
  27.3 0.0 collective-permute-done
  27.3 0.0 copy-done.1
  27.3 0.1 collective-permute-start.7
  27.3 0.0 collective-permute-done.2
  27.4 2.0 %collective-permute-start.8 = (s32[1,8]{1,0:T(1,128)S(1)}, s32[1,8]{1,0:T(1,128)S(1)}, u32[]{:S(2)}, u32[]{:S(2)}) collective-permute-start(s32[1,8]{1,0:T(1,128)S(1)} %collective-permute-done), channel_id=1, source_target_pairs={{0,1},{1,2},{2,3},{3,0},{4,5},{5,6},{6,7},{7,4},{8,9},{9,10},{10,1... | collective-permute-start | bytes 104 | tf_op jit(solution)/shard_map/ppermute | solution.py:13
  29.4 0.2 convolution_bitcast_fusion.2
  29.5 0.0 collective-permute-done.4
  29.5 0.9 %collective-permute-start.10 = (bf16[1,8,256]{2,1,0:T(8,128)(2,1)S(1)}, bf16[1,8,256]{2,1,0:T(8,128)(2,1)S(1)}, u32[]{:S(2)}, u32[]{:S(2)}) collective-permute-start(bf16[1,8,256]{2,1,0:T(8,128)(2,1)S(1)} %collective-permute-done.2), channel_id=1, source_target_pairs={{0,1},{1,2},{2,3},{3,0},{4,5},{5,6},{6,7},{7,4},{8,9},{9,10},{10,1... | collective-permute-start | bytes 12296 | tf_op jit(solution)/shard_map/ppermute | solution.py:13
  30.5 0.0 collective-permute-done.6
  30.5 0.2 convolution_bitcast_fusion.1
  30.7 0.4 rev.16
  31.1 0.4 tile.59
  31.5 0.4 slice.46
  31.8 1.3 %reshape.548 = bf16[1,2,256,511]{3,2,1,0:T(8,128)(2,1)S(1)} reshape(bf16[1,2,130816]{2,1,0:T(2,128)(2,1)S(1)} %slice.46) | data formatting | bytes 1046528 | tf_op jit(solution)/shard_map/while/body/eval_jaxpr/reshape | solution.py:25
  33.2 0.4 rev.17
  33.6 0.4 tile.62
  34.0 0.4 slice.48
  34.3 1.3 %reshape.551 = bf16[1,2,256,511]{3,2,1,0:T(8,128)(2,1)S(1)} reshape(bf16[1,2,130816]{2,1,0:T(2,128)(2,1)S(1)} %slice.48) | data formatting | bytes 1046528 | tf_op jit(solution)/shard_map/while/body/eval_jaxpr/reshape | solution.py:25
  35.7 0.0 collective-permute-done.8
  35.7 0.0 collective-permute-done.10
  35.7 0.2 convolution_bitcast_fusion
  35.9 0.4 rev.18
  36.3 0.4 tile.65
  36.7 0.4 slice.50
  37.1 1.3 %reshape.554 = bf16[1,2,256,511]{3,2,1,0:T(8,128)(2,1)S(1)} reshape(bf16[1,2,130816]{2,1,0:T(2,128)(2,1)S(1)} %slice.50) | data formatting | bytes 1046528 | tf_op jit(solution)/shard_map/reshape | solution.py:25
  38.4 0.0 collective-permute-done.3
  38.4 0.6 %collective-permute-start.11 = (bf16[1,6,256,128]{3,2,1,0:T(8,128)(2,1)}, bf16[1,6,256,128]{3,2,1,0:T(8,128)(2,1)S(1)}, u32[]{:S(2)}, u32[]{:S(2)}) collective-permute-start(bf16[1,6,256,128]{3,2,1,0:T(8,128)(2,1)} %collective-permute-done.3), channel_id=1, source_target_pairs={{0,1},{1,2},{2,3},{3,0},{4,5},{5,6},{6,7},{7,4},{8,9},{9,10},{10,1... | collective-permute-start | bytes 1179656 | tf_op jit(solution)/shard_map/ppermute | solution.py:13
  39.0 1.1 %bitcast_convert_fusion.2 = f32[6,256,128]{2,1,0:T(8,128)S(1)} fusion(bf16[1,6,256,128]{3,2,1,0:T(8,128)(2,1)} %collective-permute-done.3), kind=kLoop, calls=%fused_computation.14 | loop fusion | flops 196608 | bytes 1179648 | tf_op jit(solution)/shard_map/while/body/eval_jaxpr/convert_element_type | solution.py:37
  40.1 0.0 collective-permute-done.7
  40.1 1.0 %bitcast_convert_fusion.1 = f32[6,256,128]{2,1,0:T(8,128)S(1)} fusion(bf16[1,6,256,128]{3,2,1,0:T(8,128)(2,1)} %collective-permute-done.7), kind=kLoop, calls=%fused_computation.13 | loop fusion | flops 196608 | bytes 1179648 | tf_op jit(solution)/shard_map/while/body/eval_jaxpr/convert_element_type | solution.py:37
  41.2 0.6 %fusion.2 = f32[128]{0:T(128)S(1)} fusion(f32[6,256,128]{2,1,0:T(8,128)S(1)} %bitcast_convert_fusion.2, bf16[2,6,256,128]{3,2,1,0:T(8,128)(2,1)S(1)} %copy-done, bf16[1,2,256,511]{3,2,1,0:T(8,128)(2,1)S(1)} %reshape.548), kind=kOutput, calls=%fused_computation.5 | convolution fusion | flops 202112896 | bytes 1835520 | tf_op jit(solution)/shard_map/while/body/eval_jaxpr/setu,ecuv->sectv/dot_general | solution.py:36
  41.8 0.6 %fusion.1 = f32[128]{0:T(128)S(1)} fusion(f32[6,256,128]{2,1,0:T(8,128)S(1)} %bitcast_convert_fusion.1, bf16[2,6,256,128]{3,2,1,0:T(8,128)(2,1)S(1)} %copy-done, bf16[1,2,256,511]{3,2,1,0:T(8,128)(2,1)S(1)} %reshape.551), kind=kOutput, calls=%fused_computation.3 | convolution fusion | flops 202112896 | bytes 1835520 | tf_op jit(solution)/shard_map/while/body/eval_jaxpr/setu,ecuv->sectv/dot_general | solution.py:36
  42.5 5.0 %collective-permute-done.11 = bf16[1,6,256,128]{3,2,1,0:T(8,128)(2,1)S(1)} collective-permute-done((bf16[1,6,256,128]{3,2,1,0:T(8,128)(2,1)}, bf16[1,6,256,128]{3,2,1,0:T(8,128)(2,1)S(1)}, u32[]{:S(2)}, u32[]{:S(2)}) %collective-permute-start.11) | collective-permute-done | bytes 393248 | tf_op jit(solution)/shard_map/ppermute | solution.py:13
  47.4 0.1 bitcast_convert_fusion
  47.5 0.6 %fusion = f32[128]{0:T(128)S(1)} fusion(f32[6,256,128]{2,1,0:T(8,128)S(1)} %bitcast_convert_fusion, bf16[2,6,256,128]{3,2,1,0:T(8,128)(2,1)S(1)} %copy-done, bf16[1,2,256,511]{3,2,1,0:T(8,128)(2,1)S(1)} %reshape.554), kind=kOutput, calls=%fused_computation.1 | convolution fusion | flops 202112896 | bytes 1835520 | tf_op jit(solution)/shard_map/setu,ecuv->sectv/dot_general | solution.py:36
  48.1 8.6 %all-reduce.4 = f32[128]{0:T(128)S(1)} all-reduce(f32[128]{0:T(128)S(1)} %add_add_fusion), channel_id=2, replica_groups=mesh['vox'=8,'sta'=4] {'sta'}, use_global_device_ids=true, to_apply=%region_4.5.clone | all-reduce | flops 128 | bytes 1024
  56.7 0.6 %dynamic-slice.1 = f32[32]{0:T(128)} dynamic-slice(f32[128]{0:T(128)S(1)} %all-reduce.4, u32[]{:T(128)S(6)} %multiply.1), dynamic_slice_sizes={32} | dynamic-slice | bytes 260
  (16 shorter events, 0.2 us)
Async XLA Ops:
  0.0 14.5 %copy-start = (bf16[2,6,256,128]{3,2,1,0:T(8,128)(2,1)S(1)}, bf16[2,6,256,128]{3,2,1,0:T(8,128)(2,1)}, u32[]{:S(2)}) copy-start(bf16[2,6,256,128]{3,2,1,0:T(8,128)(2,1)} %param.6) | copy-start | bytes 2359300
  0.0 10.5 %copy-start.2 = (f32[1,8,256]{2,1,0:T(8,128)S(1)}, f32[1,8,256]{2,1,0:T(8,128)}, u32[]{:S(2)}) copy-start(f32[1,8,256]{2,1,0:T(8,128)} %param.9) | copy-start | bytes 24580
  0.0 10.5 %copy-start.3 = (s32[1,8]{1,0:T(1,128)S(1)}, s32[1,8]{1,0:T(1,128)}, u32[]{:S(2)}) copy-start(s32[1,8]{1,0:T(1,128)} %param.7) | copy-start | bytes 100
  0.8 26.6 %collective-permute-start.2 = (bf16[1,8,256]{2,1,0:T(8,128)(2,1)S(1)}, bf16[1,8,256]{2,1,0:T(8,128)(2,1)S(1)}, u32[]{:S(2)}, u32[]{:S(2)}) collective-permute-start(bf16[1,8,256]{2,1,0:T(8,128)(2,1)S(1)} %convert_element_type.72), channel_id=1, source_target_pairs={{0,1},{1,2},{2,3},{3,0},{4,5},{5,6},{6,7},{7,4},{8,9},{9,10},{10,1... | collective-permute-start | bytes 12296 | tf_op jit(solution)/shard_map/while/body/eval_jaxpr/ppermute | solution.py:13
  3.8 26.7 %collective-permute-start.6 = (bf16[1,8,256]{2,1,0:T(8,128)(2,1)S(1)}, bf16[1,8,256]{2,1,0:T(8,128)(2,1)S(1)}, u32[]{:S(2)}, u32[]{:S(2)}) collective-permute-start(bf16[1,8,256]{2,1,0:T(8,128)(2,1)S(1)} %convert_element_type.72), channel_id=1, source_target_pairs={{0,3},{1,0},{2,1},{3,2},{4,7},{5,4},{6,5},{7,6},{8,11},{9,8},{10,9... | collective-permute-start | bytes 12296 | tf_op jit(solution)/shard_map/while/body/eval_jaxpr/ppermute | solution.py:13
  4.7 10.4 %collective-permute-start.1 = (s32[1]{0:T(128)}, s32[1]{0:T(128)}, u32[]{:S(2)}, u32[]{:S(2)}) collective-permute-start(s32[1]{0:T(128)} %param.8), channel_id=1, source_target_pairs={{0,1},{1,2},{2,3},{3,0},{4,5},{5,6},{6,7},{7,4},{8,9},{9,10},{10,1... | collective-permute-start | bytes 20 | tf_op jit(solution)/shard_map/while/body/eval_jaxpr/ppermute | solution.py:13
  5.8 21.5 %collective-permute-start = (s32[1,8]{1,0:T(1,128)}, s32[1,8]{1,0:T(1,128)S(1)}, u32[]{:S(2)}, u32[]{:S(2)}) collective-permute-start(s32[1,8]{1,0:T(1,128)} %param.7), channel_id=1, source_target_pairs={{0,1},{1,2},{2,3},{3,0},{4,5},{5,6},{6,7},{7,4},{8,9},{9,10},{10,1... | collective-permute-start | bytes 104 | tf_op jit(solution)/shard_map/while/body/eval_jaxpr/ppermute | solution.py:13
  8.2 30.2 %collective-permute-start.3 = (bf16[1,6,256,128]{3,2,1,0:T(8,128)(2,1)}, bf16[1,6,256,128]{3,2,1,0:T(8,128)(2,1)}, u32[]{:S(2)}, u32[]{:S(2)}) collective-permute-start(bf16[1,6,256,128]{3,2,1,0:T(8,128)(2,1)} %param.5), channel_id=1, source_target_pairs={{0,1},{1,2},{2,3},{3,0},{4,5},{5,6},{6,7},{7,4},{8,9},{9,10},{10,1... | collective-permute-start | bytes 1179656 | tf_op jit(solution)/shard_map/while/body/eval_jaxpr/ppermute | solution.py:13
  11.9 1.3 %copy-start.4 = (u32[32]{0:T(128)S(1)}, u32[32]{0:T(128)}, u32[]{:S(2)}) copy-start(u32[32]{0:T(128)} %constant.31) | copy-start | bytes 388
  14.5 12.8 %copy-start.1 = (bf16[1,6,256,128]{3,2,1,0:T(8,128)(2,1)S(1)}, bf16[1,6,256,128]{3,2,1,0:T(8,128)(2,1)}, u32[]{:S(2)}) copy-start(bf16[1,6,256,128]{3,2,1,0:T(8,128)(2,1)} %param.5) | copy-start | bytes 1179652
  15.2 3.8 %collective-permute-start.5 = (s32[1]{0:T(128)}, s32[1]{0:T(128)}, u32[]{:S(2)}, u32[]{:S(2)}) collective-permute-start(s32[1]{0:T(128)} %param.8), channel_id=1, source_target_pairs={{0,3},{1,0},{2,1},{3,2},{4,7},{5,4},{6,5},{7,6},{8,11},{9,8},{10,9... | collective-permute-start | bytes 20 | tf_op jit(solution)/shard_map/while/body/eval_jaxpr/ppermute | solution.py:13
  19.7 4.9 %collective-permute-start.9 = (s32[1]{0:T(128)}, s32[1]{0:T(128)}, u32[]{:S(2)}, u32[]{:S(2)}) collective-permute-start(s32[1]{0:T(128)} %collective-permute-done.1), channel_id=1, source_target_pairs={{0,1},{1,2},{2,3},{3,0},{4,5},{5,6},{6,7},{7,4},{8,9},{9,10},{10,1... | collective-permute-start | bytes 20 | tf_op jit(solution)/shard_map/ppermute | solution.py:13
  24.6 5.0 %collective-permute-start.4 = (s32[1,8]{1,0:T(1,128)S(1)}, s32[1,8]{1,0:T(1,128)S(1)}, u32[]{:S(2)}, u32[]{:S(2)}) collective-permute-start(s32[1,8]{1,0:T(1,128)S(1)} %copy-done.3), channel_id=1, source_target_pairs={{0,3},{1,0},{2,1},{3,2},{4,7},{5,4},{6,5},{7,6},{8,11},{9,8},{10,9... | collective-permute-start | bytes 104 | tf_op jit(solution)/shard_map/while/body/eval_jaxpr/ppermute | solution.py:13
  27.3 12.9 %collective-permute-start.7 = (bf16[1,6,256,128]{3,2,1,0:T(8,128)(2,1)S(1)}, bf16[1,6,256,128]{3,2,1,0:T(8,128)(2,1)}, u32[]{:S(2)}, u32[]{:S(2)}) collective-permute-start(bf16[1,6,256,128]{3,2,1,0:T(8,128)(2,1)S(1)} %copy-done.1), channel_id=1, source_target_pairs={{0,3},{1,0},{2,1},{3,2},{4,7},{5,4},{6,5},{7,6},{8,11},{9,8},{10,9... | collective-permute-start | bytes 1179656 | tf_op jit(solution)/shard_map/while/body/eval_jaxpr/ppermute | solution.py:13
  27.4 8.3 %collective-permute-start.8 = (s32[1,8]{1,0:T(1,128)S(1)}, s32[1,8]{1,0:T(1,128)S(1)}, u32[]{:S(2)}, u32[]{:S(2)}) collective-permute-start(s32[1,8]{1,0:T(1,128)S(1)} %collective-permute-done), channel_id=1, source_target_pairs={{0,1},{1,2},{2,3},{3,0},{4,5},{5,6},{6,7},{7,4},{8,9},{9,10},{10,1... | collective-permute-start | bytes 104 | tf_op jit(solution)/shard_map/ppermute | solution.py:13
  29.5 6.1 %collective-permute-start.10 = (bf16[1,8,256]{2,1,0:T(8,128)(2,1)S(1)}, bf16[1,8,256]{2,1,0:T(8,128)(2,1)S(1)}, u32[]{:S(2)}, u32[]{:S(2)}) collective-permute-start(bf16[1,8,256]{2,1,0:T(8,128)(2,1)S(1)} %collective-permute-done.2), channel_id=1, source_target_pairs={{0,1},{1,2},{2,3},{3,0},{4,5},{5,6},{6,7},{7,4},{8,9},{9,10},{10,1... | collective-permute-start | bytes 12296 | tf_op jit(solution)/shard_map/ppermute | solution.py:13
  38.4 9.0 %collective-permute-start.11 = (bf16[1,6,256,128]{3,2,1,0:T(8,128)(2,1)}, bf16[1,6,256,128]{3,2,1,0:T(8,128)(2,1)S(1)}, u32[]{:S(2)}, u32[]{:S(2)}) collective-permute-start(bf16[1,6,256,128]{3,2,1,0:T(8,128)(2,1)} %collective-permute-done.3), channel_id=1, source_target_pairs={{0,1},{1,2},{2,3},{3,0},{4,5},{5,6},{6,7},{7,4},{8,9},{9,10},{10,1... | collective-permute-start | bytes 1179656 | tf_op jit(solution)/shard_map/ppermute | solution.py:13
where the time goes:
time: 57.6 us; the launch traced here: 57.3 us
  starting transfers between devices  17.8 us (31%)
  local copies, waits for them, and re-layouts  11.2 us (19%)
  waiting for transfers between devices  8.97 us (16%)
  blocking collectives  8.59 us (15%)
  other arithmetic  5.95 us (10%)
  matrix products  3.28 us (6%)
  between operations  1.59 us (3%)
    ppermute x12, starting transfers between devices, from_behind(): return lax.ppermute(x, axis, [(i, (i + by) % count) for i in range(count)])  17.8 us
    ppermute x12, waiting for transfers between devices, from_behind(): return lax.ppermute(x, axis, [(i, (i + by) % count) for i in range(count)])  8.97 us
    unnamed x1, blocking collectives  8.59 us
    reshape x4, local copies, waits for them, and re-layouts, toeplitz(): shaped = trimmed.reshape(leading + (length, width))  5.29 us
    convert_element_type x4, other arithmetic, contribution(): return jnp.sum(conv * green[:, None].astype(jnp.float32), axis=(0, 1, 2, 3))  3.23 us
    dot_general x4, matrix products, contribution(): jnp.einsum('setu,ecuv->sectv', matrix, strain, preferred_element_type=jnp...  2.53 us
    lt x4, other arithmetic, contribution(): jnp.arange(events.shape[1], dtype=jnp.int32)[None, :] < counts[:, None]  1.93 us
    another operation x8, local copies, waits for them, and re-layouts, toeplitz(): tiled = jnp.tile(flipped, reps)  1.68 us
  transfers between devices with their start and end apart: 12, of which 3 were waited for; matrix products, arithmetic and copies ran while one was open for 32% of the time, Pallas kernels for 0%

commit v1 on v0

v1 whole, which is shorter than its diff:
```python
import functools

import jax
import jax.numpy as jnp
from jax import lax
from jax.experimental import pallas as pl
from jax.experimental.pallas import tpu as pltpu
from jax.sharding import PartitionSpec as P

LANES = 128
F32 = jnp.float32
BF16 = jnp.bfloat16


def kernel(
    n, events_ref, counts_ref, resid_ref, green_hbm, strain_hbm, out_ref,
    green, strain, packed_green, packed_strain, all_comb, all_green, all_strain, adjoint,
    load_sem, send_sem, recv_sem,
):
    me = lax.axis_index("sta")
    comps, nt, vox = green.shape
    local_events = strain.shape[0]
    slots = resid_ref.shape[0]
    width = vox // n
    per_tile = LANES // width
    full = comps // per_tile
    rest = comps % per_tile
    fit = min(per_tile // rest, local_events) if rest else 1
    blocks = nt // LANES

    def peer(d):
        pair = lax.rem(me // 2 + d // 2, n // 2)
        return 2 * pair + lax.rem(me + d, 2)

    order = list(range(n - 1, 0, -1))
    load_green = pltpu.make_async_copy(green_hbm.at[0], green, load_sem.at[0])
    load_strain = pltpu.make_async_copy(strain_hbm, strain, load_sem.at[1])
    load_green.start()
    load_strain.start()

    barrier = pltpu.get_barrier_semaphore()
    for d in order:
        pl.semaphore_signal(
            barrier, inc=1, device_id={"sta": peer(d)}, device_id_type=pl.DeviceIdType.MESH
        )

    def send(kind, src, dst, d):
        copy = pltpu.make_async_remote_copy(
            src_ref=src,
            dst_ref=dst.at[me],
            send_sem=send_sem.at[kind, d],
            recv_sem=recv_sem.at[kind, me],
            device_id={"sta": peer(d)},
            device_id_type=pl.DeviceIdType.MESH,
        )
        copy.start()
        return copy

    def wait_from(kind, dst, j):
        pltpu.make_async_remote_copy(
            src_ref=dst.at[j],
            dst_ref=dst.at[j],
            send_sem=send_sem.at[kind, 0],
            recv_sem=recv_sem.at[kind, j],
            device_id={"sta": j},
            device_id_type=pl.DeviceIdType.MESH,
        ).wait_recv()

    rows = lax.broadcasted_iota(jnp.int32, (all_comb.shape[1], nt), 0)
    comb = jnp.zeros((all_comb.shape[1], nt), F32)
    for p in range(slots):
        event = jnp.where(p < counts_ref[0], events_ref[0, p], -1)
        comb = comb + jnp.where(rows == event, resid_ref[p : p + 1, :], 0.0)
    all_comb[me] = comb

    lane = lax.broadcasted_iota(jnp.int32, (LANES, LANES), 0)
    column = lax.broadcasted_iota(jnp.int32, (LANES, LANES), 1)

    def pick(j, slot):
        inside = (column >= slot * width) & (column < (slot + 1) * width)
        return inside & (lane == column + (j - slot) * width)

    def as_matrix(masks):
        return jnp.concatenate([jnp.where(m, 1.0, 0.0).astype(BF16) for m in masks], axis=0)

    def gathered(tiles, matrix):
        wide = jnp.concatenate(tiles, axis=1)
        return jnp.dot(wide, matrix[: len(tiles) * LANES], preferred_element_type=F32).astype(BF16)

    def pack_green(j, masks, matrix, dst, index):
        for a in range(full):
            dst[index, a] = gathered([green[a * per_tile + k] for k in range(per_tile)], matrix)
        if rest:
            repeated = []
            for k in range(rest):
                hit = masks[k]
                for i in range(1, fit):
                    hit = hit | masks[i * rest + k]
                repeated.append(hit)
            dst[index, full] = gathered(
                [green[full * per_tile + k] for k in range(rest)], as_matrix(repeated)
            )

    def pack_strain(matrix, dst, index):
        tile = 0
        for e in range(local_events):
            for a in range(full):
                dst[index, tile] = gathered(
                    [strain[e, a * per_tile + k] for k in range(per_tile)], matrix
                )
                tile += 1
        if rest:
            for e in range(0, local_events, fit):
                dst[index, tile] = gathered(
                    [strain[e + i, full * per_tile + k] for i in range(fit) for k in range(rest)],
                    matrix,
                )
                tile += 1

    matrices = {}
    for d in order + [0]:
        j = peer(d)
        masks = [pick(j, slot) for slot in range(per_tile)]
        matrices[d] = (j, masks, as_matrix(masks))

    load_green.wait()
    copies = []
    pl.semaphore_wait(barrier, n - 1)
    for d in order:
        copies.append(send(0, all_comb.at[me], all_comb, d))
    waiting = None
    for d in order:
        pack_green(*matrices[d], packed_green, d)
        if waiting is not None:
            copies.append(send(1, packed_green.at[waiting], all_green, waiting))
        waiting = d
    pack_green(*matrices[0], all_green, me)
    copies.append(send(1, packed_green.at[waiting], all_green, waiting))
    load_strain.wait()
    waiting = None
    for d in order:
        pack_strain(matrices[d][2], packed_strain, d)
        if waiting is not None:
            copies.append(send(2, packed_strain.at[waiting], all_strain, waiting))
        waiting = d
    pack_strain(matrices[0][2], all_strain, me)
    copies.append(send(2, packed_strain.at[waiting], all_strain, waiting))

    for d in order:
        wait_from(0, all_comb, peer(d))
    for d in order:
        wait_from(1, all_green, peer(d))

    later = column >= lane
    nothing = jnp.zeros((LANES, LANES), BF16)
    tiles = all_green.shape[1]

    @pl.loop(0, all_comb.shape[1])
    def _(e):
        total = jnp.zeros((nt, tiles * LANES), F32)
        for s in range(n):
            wave = all_comb[s, pl.ds(e, 1), :]
            turned = []
            for k in range(blocks):
                piece = jnp.broadcast_to(wave[:, k * LANES : (k + 1) * LANES], (LANES, LANES))
                turned.append(pltpu.roll(piece, 0, 1, stride=1, stride_axis=0))
            diag = [
                jnp.where(later, turned[k], turned[k - 1] if k else 0.0).astype(BF16)
                for k in range(blocks)
            ]
            matrix = jnp.concatenate(
                [
                    jnp.concatenate([nothing] * i + diag[: blocks - i], axis=1)
                    for i in range(blocks)
                ],
                axis=0,
            )
            field = jnp.concatenate([all_green[s, t] for t in range(tiles)], axis=1)
            total = total + jnp.dot(matrix, field, preferred_element_type=F32)
        adjoint[e] = total

    spot = lax.broadcasted_iota(jnp.int32, (nt, LANES), 1)

    def meet(j):
        part = jnp.zeros((1, LANES), F32)
        tile = 0
        for e in range(local_events):
            for a in range(full):
                field = all_strain[j, tile].astype(F32)
                one = adjoint[j * local_events + e, :, a * LANES : (a + 1) * LANES]
                part = part + jnp.sum(field * one, axis=0, keepdims=True)
                tile += 1
        if rest:
            for e in range(0, local_events, fit):
                field = all_strain[j, tile].astype(F32)
                one = adjoint[j * local_events + e, :, full * LANES :]
                for i in range(1, fit):
                    other = adjoint[j * local_events + e + i, :, full * LANES :]
                    one = jnp.where(spot < i * rest * width, one, other)
                part = part + jnp.sum(
                    jnp.where(spot < fit * rest * width, field * one, 0.0), axis=0, keepdims=True
                )
                tile += 1
        return part

    answer = meet(me)
    for d in order:
        j = peer(d)
        wait_from(2, all_strain, j)
        answer = answer + meet(j)
    total = answer[:, :width]
    for k in range(1, per_tile):
        total = total + answer[:, k * width : (k + 1) * width]
    out_ref[...] = total
    for copy in copies:
        copy.wait_send()


def solution(mesh):
    n = mesh.shape["sta"]

    def body(green_tensor, strain, pair_events, pair_counts, residuals):
        _, comps, nt, vox = green_tensor.shape
        local_events = strain.shape[0]
        width = vox // n
        per_tile = LANES // width
        full = comps // per_tile
        rest = comps % per_tile
        fit = min(per_tile // rest, local_events) if rest else 1
        green_tiles = full + (1 if rest else 0)
        strain_tiles = full * local_events + (local_events // fit if rest else 0)
        events = n * local_events
        out = pl.pallas_call(
            functools.partial(kernel, n),
            out_shape=jax.ShapeDtypeStruct((1, width), F32),
            in_specs=[
                pl.BlockSpec(memory_space=pltpu.SMEM),
                pl.BlockSpec(memory_space=pltpu.SMEM),
                pl.BlockSpec(memory_space=pltpu.VMEM),
                pl.BlockSpec(memory_space=pl.ANY),
                pl.BlockSpec(memory_space=pl.ANY),
            ],
            out_specs=pl.BlockSpec(memory_space=pltpu.VMEM),
            scratch_shapes=[
                pltpu.VMEM((comps, nt, vox), BF16),
                pltpu.VMEM((local_events, comps, nt, vox), BF16),
                pltpu.VMEM((n, green_tiles, nt, LANES), BF16),
                pltpu.VMEM((n, strain_tiles, nt, LANES), BF16),
                pltpu.VMEM((n, events, nt), F32),
                pltpu.VMEM((n, green_tiles, nt, LANES), BF16),
                pltpu.VMEM((n, strain_tiles, nt, LANES), BF16),
                pltpu.VMEM((events, nt, green_tiles * LANES), F32),
                pltpu.SemaphoreType.DMA((2,)),
                pltpu.SemaphoreType.DMA((3, n)),
                pltpu.SemaphoreType.DMA((3, n)),
            ],
            compiler_params=pltpu.CompilerParams(collective_id=0, has_side_effects=True),
        )(pair_events, pair_counts, residuals[0], green_tensor, strain)
        return out[0]

    in_specs = (
        P("sta", None, None, "vox"),
        P("sta", None, None, "vox"),
        P("sta", None),
        P("sta"),
        P("sta", None, None),
    )
    out_specs = P(("vox", "sta"))
    return jax.shard_map(body, mesh=mesh, in_specs=in_specs, out_specs=out_specs, check_vma=False)
```

time: 57.6 us -> 23.6 us (0.41)
  Pallas kernels: 0 us -> 21.6 us
  starting transfers between devices: 17.8 us -> 0 us
  local copies, waits for them, and re-layouts: 11.2 us -> 1.1 us
  waiting for transfers between devices: 8.97 us -> 0 us
  blocking collectives: 8.59 us -> 0 us
  other arithmetic: 5.95 us -> 0 us
  matrix products: 3.28 us -> 0 us
  between operations: 1.59 us -> 0.67 us
    pallas_call x0 -> x1, Pallas kernels: none -> 21.6 us  [body(): pl.pallas_call(functools.partial(kernel, n), out_shape=jax.ShapeDtypeStru...]
    ppermute x12 -> x0, starting transfers between devices: 17.8 us -> none  [from_behind(): return lax.ppermute(x, axis, [(i, (i + by) % count) for i in range(count)])]
    ppermute x12 -> x0, waiting for transfers between devices: 8.97 us -> none  [from_behind(): return lax.ppermute(x, axis, [(i, (i + by) % count) for i in range(count)])]
    unnamed x1 -> x0, blocking collectives: 8.59 us -> none
    reshape x4 -> x0, local copies, waits for them, and re-layouts: 5.29 us -> none  [toeplitz(): shaped = trimmed.reshape(leading + (length, width))]
    convert_element_type x5 -> x0, other arithmetic: 4.01 us -> none  [the longest x4 3.23 us: contribution(): return jnp.sum(conv * green[:, None].astype(jnp.float32), axis=(0, 1, 2, 3))]
    dot_general x8 -> x0, matrix products: 3.28 us -> none  [the longest x4 2.53 us: contribution(): jnp.einsum('setu,ecuv->sectv', matrix, strain, preferred_element_type=jnp...]
    lt x4 -> x0, other arithmetic: 1.93 us -> none  [contribution(): jnp.arange(events.shape[1], dtype=jnp.int32)[None, :] < counts[:, None]]
  transfers between devices with their start and end apart: 12 -> 0, of which waited for: 3 -> 0; matrix products, arithmetic and copies ran while one was open for 32% -> 0% of each run, Pallas kernels for 0% -> 0%
where the time goes in v1:
time: 23.6 us; the launch traced here: 23.4 us
  Pallas kernels  21.6 us (92%)
  local copies, waits for them, and re-layouts  1.1 us (5%)
  between operations  0.67 us (3%)
    pallas_call x1, Pallas kernels, body(): pl.pallas_call(functools.partial(kernel, n), out_shape=jax.ShapeDtypeStru...  21.6 us
    unnamed x3, local copies, waits for them, and re-layouts  1.1 us

profile of v1, /device:TPU:0, one launch (start us, length us, event | category | flops | bytes accessed | tf_op | source)
XLA Modules:
  0.0 23.4 jit_solution(17244198570054477074)
XLA Ops:
  0.7 21.6 %shard_map.55 = f32[1,32]{1,0:T(1,128)} custom-call(s32[1,8]{1,0:T(1,128)} %events_ref.1, s32[1]{0:T(128)S(6)} %copy.7.counts_ref, f32[8,256]{1,0:T(8,128)} %bitcast.2, bf16[1,6,256,128]{3,2,1,0:T(8,128)(2,1)} %green_hbm.1, bf16[2,6,256,128]{3,2,1,0:T(8,128)(2,1)} %strain_hbm.1), custom_call_target="tpu_custom_call" | custom-call | tf_op jit(solution)/shard_map/pallas_call | solution.py:233
  22.3 0.0 copy-start
  22.3 0.6 %copy-done = f32[1,32]{1,0:T(1,128)S(1)} copy-done((f32[1,32]{1,0:T(1,128)S(1)}, f32[1,32]{1,0:T(1,128)}, u32[]{:S(2)}) %copy-start) | copy-done | bytes 152
  22.9 0.5 %copy.8 = f32[32]{0:T(128)} copy(f32[32]{0:T(128)S(1)} %bitcast.3) | data formatting | bytes 256
Async XLA Ops:
  22.3 0.6 %copy-start = (f32[1,32]{1,0:T(1,128)S(1)}, f32[1,32]{1,0:T(1,128)}, u32[]{:S(2)}) copy-start(f32[1,32]{1,0:T(1,128)} %shard_map.55) | copy-start | bytes 388

commit v2 on v1

--- a/solution.py
+++ b/solution.py
@@ -211,8 +211,229 @@
     total = answer[:, :width]
     for k in range(1, per_tile):
         total = total + answer[:, k * width : (k + 1) * width]
-    out_ref[...] = total
+    out_ref[...] = total[0]
     for copy in copies:
+        copy.wait_send()
+
+
+def square_kernel(
+    events_ref, counts_ref, resid_ref, green_hbm, strain_hbm, out_ref,
+    green, strain, send_green, send_strain, own_green, far_green, own_strain, far_strain,
+    own_tail, far_tail, waves, own_adjoint, far_adjoint, part_out, part_in,
+    load_sem, send_sem, recv_sem,
+):
+    me = lax.axis_index("sta")
+    x, y = lax.rem(me, 2), me // 2
+    odd = lax.rem(x + y, 2)
+    beside = me + 1 - 2 * x
+    above = lax.rem(me + 2, 4)
+    first = beside + odd * (above - beside)
+    second = above + odd * (beside - above)
+    across = 3 - me
+    comps, nt, vox = green.shape
+    local_events = strain.shape[0]
+    width = vox // 4
+    per_tile = LANES // width
+    full = comps // per_tile
+    rest = comps % per_tile
+    blocks = nt // LANES
+    head = full * nt
+
+    load_green = pltpu.make_async_copy(green_hbm.at[0], green, load_sem.at[0])
+    load_strain = pltpu.make_async_copy(strain_hbm, strain, load_sem.at[1])
+    load_green.start()
+    load_strain.start()
+
+    barrier = pltpu.get_barrier_semaphore()
+    for target in (first, second, across):
+        pl.semaphore_signal(
+            barrier, inc=1, device_id={"sta": target}, device_id_type=pl.DeviceIdType.MESH
+        )
+
+    def copy_of(kind, src, dst, target):
+        return pltpu.make_async_remote_copy(
+            src_ref=src,
+            dst_ref=dst,
+            send_sem=send_sem.at[kind],
+            recv_sem=recv_sem.at[kind],
+            device_id={"sta": target},
+            device_id_type=pl.DeviceIdType.MESH,
+        )
+
+    plan = {
+        "wave1": copy_of(0, waves.at[0], waves.at[2], first),
+        "wave2": copy_of(1, waves.at[0], waves.at[1], second),
+        "wave3": copy_of(2, waves.at[0], waves.at[3], across),
+        "u0": copy_of(3, send_green.at[0], far_green.at[2], first),
+        "u1": copy_of(4, send_strain.at[0], far_strain.at[1], first),
+        "u2": copy_of(5, far_green.at[0], own_green.at[2], first),
+        "u3": copy_of(6, far_green.at[2], own_green.at[3], first),
+        "w0": copy_of(7, own_green.at[0], far_green.at[1], second),
+        "w1": copy_of(8, send_green.at[1], own_green.at[1], second),
+        "w2": copy_of(9, send_strain.at[1, 0], own_strain.at[1, 0], second),
+        "w3": copy_of(10, send_strain.at[1, 1:], own_strain.at[1, 1:], second),
+        "w4": copy_of(11, own_green.at[1], far_green.at[3], second),
+        "sum": copy_of(12, part_out, part_in, first),
+    }
+
+    events = waves.shape[1]
+    rows = lax.broadcasted_iota(jnp.int32, (events, nt), 0)
+    comb = jnp.zeros((events, nt), F32)
+    for p in range(resid_ref.shape[0]):
+        event = jnp.where(p < counts_ref[0], events_ref[0, p], -1)
+        comb = comb + jnp.where(rows == event, resid_ref[p : p + 1, :], 0.0)
+    waves[0] = comb
+
+    lane = lax.broadcasted_iota(jnp.int32, (LANES, LANES), 0)
+    column = lax.broadcasted_iota(jnp.int32, (LANES, LANES), 1)
+
+    def picker(j):
+        parts = []
+        for slot in range(per_tile):
+            inside = (column >= slot * width) & (column < (slot + 1) * width)
+            hit = inside & (lane == column + (j - slot) * width)
+            parts.append(jnp.where(hit, 1.0, 0.0).astype(BF16))
+        return jnp.concatenate(parts, axis=0)
+
+    def gathered(pieces, matrix):
+        wide = jnp.concatenate(pieces, axis=1)
+        return jnp.dot(wide, matrix, preferred_element_type=F32).astype(BF16)
+
+    def pack_green(matrix, dst, index):
+        for a in range(full):
+            dst[index, a * nt : (a + 1) * nt] = gathered(
+                [green[a * per_tile + k] for k in range(per_tile)], matrix
+            )
+        half = nt // 2
+        dst[index, head : head + half] = gathered(
+            [green[full * per_tile + k, h * half : (h + 1) * half] for h in range(2) for k in range(rest)],
+            matrix,
+        )
+
+    def pack_strain(matrix, dst, index):
+        tile = 0
+        for e in range(local_events):
+            for a in range(full):
+                dst[index, tile] = gathered(
+                    [strain[e, a * per_tile + k] for k in range(per_tile)], matrix
+                )
+                tile += 1
+        dst[index, tile] = gathered(
+            [strain[i, full * per_tile + k] for i in range(local_events) for k in range(rest)],
+            matrix,
+        )
+
+    to_across, to_me, to_second, to_first = (picker(j) for j in (across, me, second, first))
+    pl.semaphore_wait(barrier, 3)
+    for name in ("wave3", "wave1", "wave2"):
+        plan[name].start()
+    load_green.wait()
+    pack_green(to_across, send_green, 0)
+    pack_green(to_me, own_green, 0)
+    plan["u0"].start()
+    pack_green(to_second, send_green, 1)
+    plan["w0"].start()
+    load_strain.wait()
+    pack_strain(to_across, send_strain, 0)
+    plan["w1"].start()
+    pack_green(to_first, far_green, 0)
+    plan["u1"].start()
+    pack_strain(to_second, send_strain, 1)
+    plan["u2"].start()
+    pack_strain(to_first, far_strain, 0)
+    plan["w2"].start()
+    pack_strain(to_me, own_strain, 0)
+
+    later = column >= lane
+    low = column < rest * width
+    nothing = jnp.zeros((LANES, LANES), BF16)
+
+    def unfold(source, s, dst):
+        half = nt // 2
+        for b in range(half // LANES):
+            piece = source[s, head + b * LANES : head + (b + 1) * LANES].astype(F32)
+            turned = pltpu.roll(piece, LANES // 2, 1)
+            dst[s, b * LANES : (b + 1) * LANES] = jnp.where(low, piece, turned).astype(BF16)
+            dst[s, half + b * LANES : half + (b + 1) * LANES] = jnp.where(
+                low, turned, piece
+            ).astype(BF16)
+
+    def toeplitz(s, row):
+        wave = waves[s, pl.ds(row, 1), :]
+        turned = []
+        for k in range(blocks):
+            piece = jnp.broadcast_to(wave[:, k * LANES : (k + 1) * LANES], (LANES, LANES))
+            turned.append(pltpu.roll(piece, 0, 1, stride=1, stride_axis=0))
+        diag = [
+            jnp.where(later, turned[k], turned[k - 1] if k else 0.0).astype(BF16)
+            for k in range(blocks)
+        ]
+        return jnp.concatenate(
+            [jnp.concatenate([nothing] * i + diag[: blocks - i], axis=1) for i in range(blocks)],
+            axis=0,
+        )
+
+    def advance(source, tail, adjoint, partner, stations, fresh):
+        for s in stations:
+            unfold(source, s, tail)
+
+        @pl.loop(0, 2 * local_events)
+        def _(k):
+            row = me * local_events + k + (k // local_events) * (partner - me - 1) * local_events
+            total = jnp.zeros(adjoint.shape[1:], F32) if fresh else adjoint[k]
+            for s in stations:
+                field = jnp.concatenate(
+                    [source[s, a * nt : (a + 1) * nt] for a in range(full)] + [tail[s]], axis=1
+                )
+                total = total + jnp.dot(toeplitz(s, row), field, preferred_element_type=F32)
+            adjoint[k] = total
+
+    spot = lax.broadcasted_iota(jnp.int32, (nt, LANES), 1)
+
+    def meet(field, adjoint, side):
+        part = jnp.zeros((1, LANES), F32)
+        tile = 0
+        base = side * local_events
+        for e in range(local_events):
+            for a in range(full):
+                one = adjoint[base + e, :, a * LANES : (a + 1) * LANES]
+                part = part + jnp.sum(field[side, tile].astype(F32) * one, axis=0, keepdims=True)
+                tile += 1
+        one = adjoint[base, :, full * LANES :]
+        for i in range(1, local_events):
+            one = jnp.where(spot < i * rest * width, one, adjoint[base + i, :, full * LANES :])
+        return part + jnp.sum(field[side, tile].astype(F32) * one, axis=0, keepdims=True)
+
+    plan["u0"].wait_recv()
+    plan["u3"].start()
+    for name in ("wave1", "wave2", "wave3", "w0"):
+        plan[name].wait_recv()
+    advance(far_green, far_tail, far_adjoint, second, (0, 1, 2), True)
+    plan["w1"].wait_recv()
+    plan["w4"].start()
+    plan["w3"].start()
+    advance(own_green, own_tail, own_adjoint, first, (0, 1), True)
+    plan["w4"].wait_recv()
+    advance(far_green, far_tail, far_adjoint, second, (3,), False)
+    part = meet(far_strain, far_adjoint, 0)
+    plan["u1"].wait_recv()
+    part_out[...] = part + meet(far_strain, far_adjoint, 1)
+    plan["u2"].wait_recv()
+    advance(own_green, own_tail, own_adjoint, first, (2,), False)
+    plan["sum"].start()
+    plan["u3"].wait_recv()
+    advance(own_green, own_tail, own_adjoint, first, (3,), False)
+    answer = meet(own_strain, own_adjoint, 0)
+    plan["w2"].wait_recv()
+    plan["w3"].wait_recv()
+    answer = answer + meet(own_strain, own_adjoint, 1)
+    plan["sum"].wait_recv()
+    answer = answer + part_in[...]
+    total = answer[:, :width]
+    for k in range(1, per_tile):
+        total = total + answer[:, k * width : (k + 1) * width]
+    out_ref[...] = total[0]
+    for copy in plan.values():
         copy.wait_send()
 
 
@@ -230,18 +451,32 @@
         green_tiles = full + (1 if rest else 0)
         strain_tiles = full * local_events + (local_events // fit if rest else 0)
         events = n * local_events
-        out = pl.pallas_call(
-            functools.partial(kernel, n),
-            out_shape=jax.ShapeDtypeStruct((1, width), F32),
-            in_specs=[
-                pl.BlockSpec(memory_space=pltpu.SMEM),
-                pl.BlockSpec(memory_space=pltpu.SMEM),
-                pl.BlockSpec(memory_space=pltpu.VMEM),
-                pl.BlockSpec(memory_space=pl.ANY),
-                pl.BlockSpec(memory_space=pl.ANY),
-            ],
-            out_specs=pl.BlockSpec(memory_space=pltpu.VMEM),
-            scratch_shapes=[
+        packed = full * nt + nt // 2
+        if n == 4 and 2 * rest == per_tile and local_events * rest == per_tile:
+            steps = square_kernel
+            scratch = [
+                pltpu.VMEM((comps, nt, vox), BF16),
+                pltpu.VMEM((local_events, comps, nt, vox), BF16),
+                pltpu.VMEM((2, packed, LANES), BF16),
+                pltpu.VMEM((2, strain_tiles, nt, LANES), BF16),
+                pltpu.VMEM((4, packed, LANES), BF16),
+                pltpu.VMEM((4, packed, LANES), BF16),
+                pltpu.VMEM((2, strain_tiles, nt, LANES), BF16),
+                pltpu.VMEM((2, strain_tiles, nt, LANES), BF16),
+                pltpu.VMEM((4, nt, LANES), BF16),
+                pltpu.VMEM((4, nt, LANES), BF16),
+                pltpu.VMEM((4, events, nt), F32),
+                pltpu.VMEM((2 * local_events, nt, green_tiles * LANES), F32),
+                pltpu.VMEM((2 * local_events, nt, green_tiles * LANES), F32),
+                pltpu.VMEM((1, LANES), F32),
+                pltpu.VMEM((1, LANES), F32),
+                pltpu.SemaphoreType.DMA((2,)),
+                pltpu.SemaphoreType.DMA((13,)),
+                pltpu.SemaphoreType.DMA((13,)),
+            ]
+        else:
+            steps = functools.partial(kernel, n)
+            scratch = [
                 pltpu.VMEM((comps, nt, vox), BF16),
                 pltpu.VMEM((local_events, comps, nt, vox), BF16),
                 pltpu.VMEM((n, green_tiles, nt, LANES), BF16),
@@ -253,10 +488,21 @@
                 pltpu.SemaphoreType.DMA((2,)),
                 pltpu.SemaphoreType.DMA((3, n)),
                 pltpu.SemaphoreType.DMA((3, n)),
+            ]
+        return pl.pallas_call(
+            steps,
+            out_shape=jax.ShapeDtypeStruct((width,), F32),
+            in_specs=[
+                pl.BlockSpec(memory_space=pltpu.SMEM),
+                pl.BlockSpec(memory_space=pltpu.SMEM),
+                pl.BlockSpec(memory_space=pltpu.VMEM),
+                pl.BlockSpec(memory_space=pl.ANY),
+                pl.BlockSpec(memory_space=pl.ANY),
             ],
+            out_specs=pl.BlockSpec(memory_space=pltpu.VMEM),
+            scratch_shapes=scratch,
             compiler_params=pltpu.CompilerParams(collective_id=0, has_side_effects=True),
         )(pair_events, pair_counts, residuals[0], green_tensor, strain)
-        return out[0]
 
     in_specs = (
         P("sta", None, None, "vox"),

time: 23.6 us -> 23.8 us (level)
    unnamed x3 -> x1, local copies, waits for them, and re-layouts: 1.1 us -> 1.19 us
where the time goes in v2:
time: 23.8 us; the launch traced here: 23.6 us
  Pallas kernels  21.7 us (91%)
  local copies, waits for them, and re-layouts  1.19 us (5%)
  between operations  0.66 us (3%)
    pallas_call x1, Pallas kernels, body(): pl.pallas_call(steps, out_shape=jax.ShapeDtypeStruct((width,), F32), in_s...  21.7 us
    unnamed x1, local copies, waits for them, and re-layouts  1.19 us

profile of v2, /device:TPU:0, one launch (start us, length us, event | category | flops | bytes accessed | tf_op | source)
XLA Modules:
  0.0 23.6 jit_solution(14049642005358952311)
XLA Ops:
  0.7 21.7 %shard_map.55 = f32[32]{0:T(128)} custom-call(s32[1,8]{1,0:T(1,128)} %events_ref.1, s32[1]{0:T(128)S(6)} %copy.7.counts_ref, f32[8,256]{1,0:T(8,128)} %bitcast.1, bf16[1,6,256,128]{3,2,1,0:T(8,128)(2,1)} %green_hbm.1, bf16[2,6,256,128]{3,2,1,0:T(8,128)(2,1)} %strain_hbm.1), custom_call_target="tpu_custom_call" | custom-call | tf_op jit(solution)/shard_map/pallas_call | solution.py:492
  22.4 1.2 %copy.8 = f32[32]{0:T(128)} copy(f32[32]{0:T(128)} %shard_map.55) | data formatting | bytes 256

commit v3 on v2

--- a/solution.py
+++ b/solution.py
@@ -270,10 +270,9 @@
         "u3": copy_of(6, far_green.at[2], own_green.at[3], first),
         "w0": copy_of(7, own_green.at[0], far_green.at[1], second),
         "w1": copy_of(8, send_green.at[1], own_green.at[1], second),
-        "w2": copy_of(9, send_strain.at[1, 0], own_strain.at[1, 0], second),
-        "w3": copy_of(10, send_strain.at[1, 1:], own_strain.at[1, 1:], second),
-        "w4": copy_of(11, own_green.at[1], far_green.at[3], second),
-        "sum": copy_of(12, part_out, part_in, first),
+        "w2": copy_of(9, send_strain.at[1], own_strain.at[1], second),
+        "w4": copy_of(10, own_green.at[1], far_green.at[3], second),
+        "sum": copy_of(11, part_out, part_in, first),
     }
 
     events = waves.shape[1]
@@ -323,26 +322,24 @@
             matrix,
         )
 
-    to_across, to_me, to_second, to_first = (picker(j) for j in (across, me, second, first))
+    to_across, to_second = picker(across), picker(second)
+    load_green.wait()
+    pack_green(to_across, send_green, 0)
+    pack_green(to_second, send_green, 1)
+    to_me, to_first = picker(me), picker(first)
     pl.semaphore_wait(barrier, 3)
+    plan["u0"].start()
+    plan["w1"].start()
     for name in ("wave3", "wave1", "wave2"):
         plan[name].start()
-    load_green.wait()
-    pack_green(to_across, send_green, 0)
-    pack_green(to_me, own_green, 0)
-    plan["u0"].start()
-    pack_green(to_second, send_green, 1)
-    plan["w0"].start()
     load_strain.wait()
     pack_strain(to_across, send_strain, 0)
-    plan["w1"].start()
+    pack_green(to_me, own_green, 0)
+    plan["u1"].start()
     pack_green(to_first, far_green, 0)
-    plan["u1"].start()
+    plan["w0"].start()
     pack_strain(to_second, send_strain, 1)
     plan["u2"].start()
-    pack_strain(to_first, far_strain, 0)
-    plan["w2"].start()
-    pack_strain(to_me, own_strain, 0)
 
     later = column >= lane
     low = column < rest * width
@@ -406,13 +403,16 @@
 
     plan["u0"].wait_recv()
     plan["u3"].start()
-    for name in ("wave1", "wave2", "wave3", "w0"):
-        plan[name].wait_recv()
-    advance(far_green, far_tail, far_adjoint, second, (0, 1, 2), True)
     plan["w1"].wait_recv()
     plan["w4"].start()
-    plan["w3"].start()
+    plan["w2"].start()
+    pack_strain(to_first, far_strain, 0)
+    pack_strain(to_me, own_strain, 0)
+    for name in ("wave1", "wave2", "wave3"):
+        plan[name].wait_recv()
     advance(own_green, own_tail, own_adjoint, first, (0, 1), True)
+    plan["w0"].wait_recv()
+    advance(far_green, far_tail, far_adjoint, second, (0, 1, 2), True)
     plan["w4"].wait_recv()
     advance(far_green, far_tail, far_adjoint, second, (3,), False)
     part = meet(far_strain, far_adjoint, 0)
@@ -425,7 +425,6 @@
     advance(own_green, own_tail, own_adjoint, first, (3,), False)
     answer = meet(own_strain, own_adjoint, 0)
     plan["w2"].wait_recv()
-    plan["w3"].wait_recv()
     answer = answer + meet(own_strain, own_adjoint, 1)
     plan["sum"].wait_recv()
     answer = answer + part_in[...]
@@ -471,8 +470,8 @@
                 pltpu.VMEM((1, LANES), F32),
                 pltpu.VMEM((1, LANES), F32),
                 pltpu.SemaphoreType.DMA((2,)),
-                pltpu.SemaphoreType.DMA((13,)),
-                pltpu.SemaphoreType.DMA((13,)),
+                pltpu.SemaphoreType.DMA((12,)),
+                pltpu.SemaphoreType.DMA((12,)),
             ]
         else:
             steps = functools.partial(kernel, n)

time: 23.8 us -> 22.5 us (0.945)
  Pallas kernels: 21.7 us -> 20.4 us
    pallas_call x1, Pallas kernels: 21.7 us -> 20.4 us  [body(): pl.pallas_call(steps, out_shape=jax.ShapeDtypeStruct((width,), F32), in_s...]
where the time goes in v3:
time: 22.5 us; the launch traced here: 22.2 us
  Pallas kernels  20.4 us (91%)
  local copies, waits for them, and re-layouts  1.19 us (5%)
  between operations  0.66 us (3%)
    pallas_call x1, Pallas kernels, body(): pl.pallas_call(steps, out_shape=jax.ShapeDtypeStruct((width,), F32), in_s...  20.4 us
    unnamed x1, local copies, waits for them, and re-layouts  1.19 us

profile of v3, /device:TPU:0, one launch (start us, length us, event | category | flops | bytes accessed | tf_op | source)
XLA Modules:
  0.0 22.2 jit_solution(11258413603245625632)
XLA Ops:
  0.7 20.4 %shard_map.55 = f32[32]{0:T(128)} custom-call(s32[1,8]{1,0:T(1,128)} %events_ref.1, s32[1]{0:T(128)S(6)} %copy.7.counts_ref, f32[8,256]{1,0:T(8,128)} %bitcast.1, bf16[1,6,256,128]{3,2,1,0:T(8,128)(2,1)} %green_hbm.1, bf16[2,6,256,128]{3,2,1,0:T(8,128)(2,1)} %strain_hbm.1), custom_call_target="tpu_custom_call" | custom-call | tf_op jit(solution)/shard_map/pallas_call | solution.py:491
  21.0 1.2 %copy.8 = f32[32]{0:T(128)} copy(f32[32]{0:T(128)} %shard_map.55) | data formatting | bytes 256

commit v4 on v3

--- a/solution.py
+++ b/solution.py
@@ -219,7 +219,7 @@
 def square_kernel(
     events_ref, counts_ref, resid_ref, green_hbm, strain_hbm, out_ref,
     green, strain, send_green, send_strain, own_green, far_green, own_strain, far_strain,
-    own_tail, far_tail, waves, own_adjoint, far_adjoint, part_out, part_in,
+    own_tail, far_tail, waves, table, own_adjoint, far_adjoint, part_out, part_in,
     load_sem, send_sem, recv_sem,
 ):
     me = lax.axis_index("sta")
@@ -270,7 +270,8 @@
         "u3": copy_of(6, far_green.at[2], own_green.at[3], first),
         "w0": copy_of(7, own_green.at[0], far_green.at[1], second),
         "w1": copy_of(8, send_green.at[1], own_green.at[1], second),
-        "w2": copy_of(9, send_strain.at[1], own_strain.at[1], second),
+        "w2": copy_of(9, send_strain.at[1, 0], own_strain.at[1, 0], second),
+        "w3": copy_of(12, send_strain.at[1, 1:], own_strain.at[1, 1:], second),
         "w4": copy_of(10, own_green.at[1], far_green.at[3], second),
         "sum": copy_of(11, part_out, part_in, first),
     }
@@ -281,7 +282,7 @@
     for p in range(resid_ref.shape[0]):
         event = jnp.where(p < counts_ref[0], events_ref[0, p], -1)
         comb = comb + jnp.where(rows == event, resid_ref[p : p + 1, :], 0.0)
-    waves[0] = comb
+    waves[0] = comb.astype(BF16)
 
     lane = lax.broadcasted_iota(jnp.int32, (LANES, LANES), 0)
     column = lax.broadcasted_iota(jnp.int32, (LANES, LANES), 1)
@@ -356,7 +357,7 @@
             ).astype(BF16)
 
     def toeplitz(s, row):
-        wave = waves[s, pl.ds(row, 1), :]
+        wave = table[s, pl.ds(row, 1), :]
         turned = []
         for k in range(blocks):
             piece = jnp.broadcast_to(wave[:, k * LANES : (k + 1) * LANES], (LANES, LANES))
@@ -401,15 +402,17 @@
             one = jnp.where(spot < i * rest * width, one, adjoint[base + i, :, full * LANES :])
         return part + jnp.sum(field[side, tile].astype(F32) * one, axis=0, keepdims=True)
 
+    pack_strain(to_first, far_strain, 0)
+    plan["w2"].start()
     plan["u0"].wait_recv()
     plan["u3"].start()
     plan["w1"].wait_recv()
     plan["w4"].start()
-    plan["w2"].start()
-    pack_strain(to_first, far_strain, 0)
+    plan["w3"].start()
     pack_strain(to_me, own_strain, 0)
     for name in ("wave1", "wave2", "wave3"):
         plan[name].wait_recv()
+    table[...] = waves[...].astype(F32)
     advance(own_green, own_tail, own_adjoint, first, (0, 1), True)
     plan["w0"].wait_recv()
     advance(far_green, far_tail, far_adjoint, second, (0, 1, 2), True)
@@ -425,6 +428,7 @@
     advance(own_green, own_tail, own_adjoint, first, (3,), False)
     answer = meet(own_strain, own_adjoint, 0)
     plan["w2"].wait_recv()
+    plan["w3"].wait_recv()
     answer = answer + meet(own_strain, own_adjoint, 1)
     plan["sum"].wait_recv()
     answer = answer + part_in[...]
@@ -464,14 +468,15 @@
                 pltpu.VMEM((2, strain_tiles, nt, LANES), BF16),
                 pltpu.VMEM((4, nt, LANES), BF16),
                 pltpu.VMEM((4, nt, LANES), BF16),
+                pltpu.VMEM((4, events, nt), BF16),
                 pltpu.VMEM((4, events, nt), F32),
                 pltpu.VMEM((2 * local_events, nt, green_tiles * LANES), F32),
                 pltpu.VMEM((2 * local_events, nt, green_tiles * LANES), F32),
                 pltpu.VMEM((1, LANES), F32),
                 pltpu.VMEM((1, LANES), F32),
                 pltpu.SemaphoreType.DMA((2,)),
-                pltpu.SemaphoreType.DMA((12,)),
-                pltpu.SemaphoreType.DMA((12,)),
+                pltpu.SemaphoreType.DMA((13,)),
+                pltpu.SemaphoreType.DMA((13,)),
             ]
         else:
             steps = functools.partial(kernel, n)

time: 22.5 us -> 22.9 us (1.018)
  Pallas kernels: 20.4 us -> 20.9 us
    pallas_call x1, Pallas kernels: 20.4 us -> 20.9 us  [body(): pl.pallas_call(steps, out_shape=jax.ShapeDtypeStruct((width,), F32), in_s...]
where the time goes in v4:
time: 22.9 us; the launch traced here: 22.7 us
  Pallas kernels  20.9 us (91%)
  local copies, waits for them, and re-layouts  1.19 us (5%)
  between operations  0.66 us (3%)
    pallas_call x1, Pallas kernels, body(): pl.pallas_call(steps, out_shape=jax.ShapeDtypeStruct((width,), F32), in_s...  20.9 us
    unnamed x1, local copies, waits for them, and re-layouts  1.19 us

profile of v4, /device:TPU:0, one launch (start us, length us, event | category | flops | bytes accessed | tf_op | source)
XLA Modules:
  0.0 22.7 jit_solution(3294144804406445467)
XLA Ops:
  0.7 20.9 %shard_map.55 = f32[32]{0:T(128)} custom-call(s32[1,8]{1,0:T(1,128)} %events_ref.1, s32[1]{0:T(128)S(6)} %copy.7.counts_ref, f32[8,256]{1,0:T(8,128)} %bitcast.1, bf16[1,6,256,128]{3,2,1,0:T(8,128)(2,1)} %green_hbm.1, bf16[2,6,256,128]{3,2,1,0:T(8,128)(2,1)} %strain_hbm.1), custom_call_target="tpu_custom_call" | custom-call | tf_op jit(solution)/shard_map/pallas_call | solution.py:496
  21.5 1.2 %copy.8 = f32[32]{0:T(128)} copy(f32[32]{0:T(128)} %shard_map.55) | data formatting | bytes 256
